TPU v7x, 128 devices: a whole 4x4x4 slice. The times are simulated.
128 devices in a mesh: data: 1, col: 64 (over z, y, x), row: 2 (over core).
Axes of the slice: x: 4, y: 4, z: 4, core: 2. Of those that a mesh axis runs over, the one named last changes fastest.
Arguments:
- pair_rep: bfloat16 [1024, 1024, 64], P(('data', 'row'), 'col')
- res_mask: int32 [1024], P('data')
- ln_gamma: float32 [64], replicated
- ln_beta: float32 [64], replicated
- w_q: bfloat16 [64, 64], replicated
- w_k: bfloat16 [64, 64], replicated
- w_v: bfloat16 [64, 64], replicated
- w_b: bfloat16 [64, 4], replicated
- w_g: bfloat16 [64, 64], replicated
- w_o: bfloat16 [64, 64], replicated
Outputs:
- output: bfloat16 [1024, 1024, 64], P(('data', 'row'), 'col')
All inputs are finite; a program needn't handle non-finite values.
Results may differ from a plain program's by a relative error of at most 0.00643641.
Values are sent between devices in bfloat16 or wider.
A program may use at most 1 GiB of HBM per device.

v0:
```python
import math
import jax
import jax.numpy as jnp
from jax import lax
from jax.sharding import PartitionSpec as P

LN_EPS = 1e-5
MASK_FILL = -1e9


def norm_and_project(pair_tile, ln_gamma, ln_beta, w_q, w_k, w_v, w_b, w_g):
    n_chan = pair_tile.shape[-1]
    heads = w_b.shape[1]
    head_dim = w_q.shape[1] // heads
    pair_f32 = pair_tile.astype(jnp.float32)
    mean = jnp.mean(pair_f32, axis=-1, keepdims=True)
    centred = pair_f32 - mean
    variance = jnp.mean(centred * centred, axis=-1, keepdims=True)
    normed = (centred * lax.rsqrt(variance + LN_EPS) * ln_gamma + ln_beta).astype(jnp.bfloat16)
    query = (jnp.einsum('ijc,chd->jhid', normed, w_q.reshape(n_chan, heads, head_dim), preferred_element_type=jnp.float32) * (1.0 / math.sqrt(head_dim))).astype(jnp.bfloat16)
    w_kv = jnp.stack([w_k.reshape(n_chan, heads, head_dim), w_v.reshape(n_chan, heads, head_dim)])
    kv_pair = jnp.einsum('ijc,echd->ejhid', normed, w_kv, preferred_element_type=jnp.float32).astype(jnp.bfloat16)
    gate = jax.nn.sigmoid(jnp.einsum('ijc,chd->jhid', normed, w_g.reshape(n_chan, heads, head_dim), preferred_element_type=jnp.float32))
    bias_tile = jnp.einsum('ijc,ch->ijh', normed, w_b, preferred_element_type=jnp.float32).astype(jnp.bfloat16)
    return pair_f32, query, kv_pair, gate, bias_tile


def bias_strip(bias_tile):
    full_cols = lax.all_gather(bias_tile, 'col', axis=1, tiled=True)
    own_rows = lax.all_to_all(full_cols, 'row', 1, 0, tiled=True)
    return jnp.transpose(own_rows, (2, 1, 0))


def attend_block(state, query, kv_blk, bias_blk, fill_blk):
    run_max, run_sum, out_acc = state
    logits = jnp.einsum('jhid,jhkd->jhik', query, kv_blk[0], preferred_element_type=jnp.float32) + bias_blk[None] + fill_blk
    new_max = jnp.maximum(run_max, jnp.max(logits, axis=-1))
    rescale = jnp.exp(run_max - new_max)
    p_exp = jnp.exp(logits - new_max[..., None])
    run_sum = run_sum * rescale + jnp.sum(p_exp, axis=-1)
    out_acc = out_acc * rescale[..., None] + jnp.einsum('jhik,jhkd->jhid', p_exp.astype(jnp.bfloat16), kv_blk[1], preferred_element_type=jnp.float32)
    return new_max, run_sum, out_acc


def finish(state, gate, pair_f32, w_o):
    run_max, run_sum, out_acc = state
    heads = gate.shape[1]
    head_dim = gate.shape[3]
    gated = (gate * (out_acc / run_sum[..., None])).astype(jnp.bfloat16)
    update = jnp.einsum('jhid,hdc->ijc', gated, w_o.reshape(heads, head_dim, w_o.shape[1]), preferred_element_type=jnp.float32)
    return (pair_f32 + update).astype(jnp.bfloat16)


def solution(mesh):
    rows = mesh.shape['row']
    next_hop = [(src_id, (src_id + 1) % rows) for src_id in range(rows)]

    def body(pair_tile, res_mask, ln_gamma, ln_beta, w_q, w_k, w_v, w_b, w_g, w_o):
        pair_f32, query, kv_pair, gate, bias_tile = norm_and_project(pair_tile, ln_gamma, ln_beta, w_q, w_k, w_v, w_b, w_g)
        strip = bias_strip(bias_tile)
        key_fill = jnp.where(res_mask > 0, 0.0, MASK_FILL).astype(jnp.float32)
        block = pair_tile.shape[0]
        my_row = lax.axis_index('row')

        def fold(step, state, kv_blk):
            key_lo = ((my_row - step) % rows) * block
            bias_blk = lax.dynamic_slice_in_dim(strip, key_lo, block, axis=2)
            fill_blk = lax.dynamic_slice_in_dim(key_fill, key_lo, block)
            return attend_block(state, query, kv_blk, bias_blk, fill_blk)

        stat_shape = query.shape[:3]
        state = (jnp.full(stat_shape, -jnp.inf, jnp.float32), jnp.zeros(stat_shape, jnp.float32), jnp.zeros(query.shape, jnp.float32))
        state = fold(0, state, kv_pair)

        def shift_step(step, carry):
            cur_state, kv_blk = carry
            kv_blk = lax.ppermute(kv_blk, 'row', next_hop)
            return fold(step, cur_state, kv_blk), kv_blk

        state, kv_last = lax.fori_loop(1, rows, shift_step, (state, kv_pair))
        return finish(state, gate, pair_f32, w_o)

    tile_spec = P(('data', 'row'), 'col', None)
    return jax.shard_map(body, mesh=mesh, in_specs=(tile_spec, P('data'), P(), P(), P(), P(), P(), P(), P(), P()), out_specs=tile_spec, check_vma=False)
```

profile of v0, /device:TPU:1, one launch (start us, length us, event | category | flops | bytes accessed | tf_op | source)
XLA Modules:
  0.0 262.9 jit_solution(15956120720811545851)
XLA Ops:
  6.5 0.0 all-gather.2.cloned.1.call-start
  6.6 1.4 convert_reduce_fusion
  8.0 0.0 copy-start.9
  8.0 0.0 copy-start.10
  8.0 0.0 copy-start.11
  8.1 1.6 fusion.12
  9.7 1.7 fusion.15
  11.3 0.9 convolution_convert_fusion
  12.2 0.0 all-gather.2.cloned.1.call-update
  12.2 0.0 copy-done.7
  12.3 0.1 copy.27
  12.4 0.1 copy.26
  12.4 0.7 convert_bitcast_fusion.2
  13.1 1.4 collective-permute-start
  14.6 0.1 copy.25
  14.7 0.1 copy.24
  14.8 0.1 fusion.40
  14.9 1.4 fusion.20
  16.3 1.6 slice_bitcast_fusion.2
  17.9 1.8 fusion.23
  19.7 0.0 collective-permute-done
  19.7 3.1 %slice_bitcast_fusion = (bf16[16,4,512,16]{2,3,0,1:T(8,128)(2,1)}, bf16[16,4,512,16]{2,3,0,1:T(8,128)(2,1)}) fusion(bf16[2,16,4,512,16]{3,4,1,2,0:T(8,128)(2,1)} %collective-permute-done), kind=kLoop, calls=%fused_computation.30 | loop fusion | bytes 4194304 | tf_op jit(solution)/shard_map/while/body/eval_jaxpr/squeeze | solution.py:41
  22.8 59.2 %all-gather.2.cloned.1.call-done = bf16[512,1024,4]{0,2,1:T(4,128)(2,1)} async-done(((bf16[512,16,4]{0,2,1:T(4,128)(2,1)}), bf16[512,1024,4]{0,2,1:T(4,128)(2,1)}) %all-gather.2.cloned.1.call-update) | async-done | bytes 4194320 | tf_op jit(solution)/shard_map/all_gather | solution.py:29
  82.0 13.9 %all_to_all.18 = bf16[512,1024,4]{0,2,1:T(4,128)(2,1)} all-to-all(bf16[512,1024,4]{0,2,1:T(4,128)(2,1)} %all-gather.2.cloned.1.call-done), channel_id=1, replica_groups=mesh['data'=1,'col'=64,'row'=2] {'row'}, dimensions={1} | all-to-all | bytes 8388608 | tf_op jit(solution)/shard_map/all_to_all | solution.py:30
  95.9 7.5 %copy.29 = bf16[2,512,512,4]{2,1,0,3:T(8,128)(2,1)} copy(bf16[2,512,512,4]{1,3,2,0:T(4,128)(2,1)} %bitcast.70) | data formatting | bytes 8388608 | tf_op jit(solution)/shard_map/all_to_all | solution.py:30
  103.3 3.1 %convert_bitcast_fusion = (f32[4,512,512]{1,2,0:T(8,128)S(1)}, f32[4,512,512]{1,2,0:T(8,128)S(1)}) fusion(bf16[1024,512,4]{1,0,2:T(8,128)(2,1)} %bitcast.69, s32[]{:T(128)S(6)} %select_n.30, s32[]{:T(128)S(6)} %select_n.27), kind=kLoop, calls=%fused_computation.12 | loop fusion | flops 2097152 | bytes 12582920 | tf_op jit(solution)/shard_map/while/body/eval_jaxpr/convert_element_type | solution.py:36
  106.5 24.7 %fusion.1 = (f32[16,4,512]{2,1,0:T(4,128)S(1)}, f32[16,4,512,512]{2,3,1,0:T(8,128)}) fusion(f32[512]{0:T(512)S(1)} %get-tuple-element.44, f32[4,512,512]{1,2,0:T(8,128)S(1)} %get-tuple-element.25, bf16[16,4,512,16]{2,3,1,0:T(8,128)(2,1)S(1)} %copy-done.3, bf16[16,4,512,16]{2,3,0,1:T(8,128)(2,1)S(1)} %copy-done.5), kind=kOutput, calls=%fused_computation.5 | convolution fusion | flops 587169792 | bytes 73533440 | tf_op jit(solution)/shard_map/while/body/eval_jaxpr/jhid,jhkd->jhik/dot_general | solution.py:36
  131.3 24.4 %fusion = (f32[16,4,512]{2,1,0:T(4,128)S(1)}, f32[16,4,512,512]{2,3,1,0:T(8,128)}) fusion(f32[512]{0:T(512)S(1)} %get-tuple-element.45, f32[4,512,512]{1,2,0:T(8,128)S(1)} %get-tuple-element.26, bf16[16,4,512,16]{2,3,1,0:T(8,128)(2,1)S(1)} %copy-done.3, bf16[16,4,512,16]{2,3,0,1:T(8,128)(2,1)S(1)} %copy-done.4), kind=kOutput, calls=%fused_computation.4 | convolution fusion | flops 587169792 | bytes 73533440 | tf_op jit(solution)/shard_map/jhid,jhkd->jhik/dot_general | solution.py:36
  155.7 26.2 %fusion.8 = f32[16,4,512,16]{2,3,1,0:T(8,128)} fusion(f32[16,4,512,512]{2,3,1,0:T(8,128)} %get-tuple-element.47, f32[16,4,512]{2,1,0:T(4,128)S(1)} %get-tuple-element.46, f32[512]{0:T(512)S(1)} %get-tuple-element.45, f32[4,512,512]{1,2,0:T(8,128)} %copy-done.2, bf16[16,4,512,16]{2,3,0,1:T(8,128)(2,1)S(1)} %copy-done.6), kind=kOutput, calls=%fused_computation.11 | convolution fusion | flops 603979776 | bytes 74582016 | tf_op jit(solution)/shard_map/jhik,jhkd->jhid/dot_general | solution.py:41
  181.9 45.5 %fusion.2 = (f32[16,4,512]{2,1,0:T(4,128)S(1)}, f32[16,4,512]{2,1,0:T(4,128)S(1)}) fusion(f32[16,4,512,512]{2,3,1,0:T(8,128)} %get-tuple-element.47, f32[16,4,512]{2,1,0:T(4,128)S(1)} %get-tuple-element.46, f32[512]{0:T(512)S(1)} %get-tuple-element.45, f32[4,512,512]{1,2,0:T(8,128)} %copy-done.2, f32[16,4,512]{2,1,0:T(4,128)S(1)} %max.14, ...), kind=kLoop, calls=%fused_computation.6 | loop fusion | flops 134152192 | bytes 143134720 | tf_op jit(solution)/shard_map/reduce_sum | solution.py:40
  227.4 0.1 multiply_add_fusion
  227.6 28.5 %fusion.16 = bf16[512,16,64]{0,2,1:T(8,128)(2,1)} fusion(bf16[512,16,64]{0,2,1:T(8,128)(2,1)} %param.10, bf16[4,16,64,1]{2,1,0,3:T(8,128)(2,1)S(1)} %bitcast.68, f32[16,4,512,16]{2,3,1,0:T(8,128)} %fusion.8, f32[512,16,4,16]{0,3,2,1:T(8,128)} %fusion.23, f32[16,4,512,512]{2,3,1,0:T(8,128)} %get-tuple-element.49, f32[16,4,512]{2,1,0:T(4,128)S(1)} %max.14, ...), kind=kOutput, calls=%fused_computation.23 | convolution fusion | flops 677380096 | bytes 79177728 | tf_op jit(solution)/shard_map/jhid,hdc->ijc/dot_general | solution.py:50
  (26 shorter events, 0.1 us)
Async XLA Ops:
  6.5 221.0 %copy-start = (bf16[64,64]{1,0:T(8,128)(2,1)S(1)}, bf16[64,64]{1,0:T(8,128)(2,1)}, u32[]{:S(2)}) copy-start(bf16[64,64]{1,0:T(8,128)(2,1)} %param.19) | copy-start | bytes 24580
  6.5 4.8 %copy-start.12 = (bf16[64,4]{0,1:T(4,128)(2,1)S(1)}, bf16[64,4]{0,1:T(4,128)(2,1)}, u32[]{:S(2)}) copy-start(bf16[64,4]{0,1:T(4,128)(2,1)} %param.17) | copy-start | bytes 1540
  6.5 5.7 %copy-start.7 = (bf16[64,64]{1,0:T(8,128)(2,1)S(1)}, bf16[64,64]{1,0:T(8,128)(2,1)}, u32[]{:S(2)}) copy-start(bf16[64,64]{1,0:T(8,128)(2,1)} %param.16) | copy-start | bytes 24580
  6.5 5.8 %copy-start.8 = (bf16[64,64]{1,0:T(8,128)(2,1)S(1)}, bf16[64,64]{1,0:T(8,128)(2,1)}, u32[]{:S(2)}) copy-start(bf16[64,64]{1,0:T(8,128)(2,1)} %param.15) | copy-start | bytes 24580
  6.5 75.5 %all-gather.2.cloned.1.call-start = ((), (), s32[]{:S(2)}) async-start(), calls=%async_computation.1 | async-start | bytes 4259840 | tf_op jit(solution)/shard_map/all_gather | solution.py:29
  8.0 6.6 %copy-start.9 = (bf16[64,64]{1,0:T(8,128)(2,1)S(1)}, bf16[64,64]{1,0:T(8,128)(2,1)}, u32[]{:S(2)}) copy-start(bf16[64,64]{1,0:T(8,128)(2,1)} %param.14) | copy-start | bytes 24580
  8.0 6.6 %copy-start.10 = (bf16[64,64]{1,0:T(8,128)(2,1)S(1)}, bf16[64,64]{1,0:T(8,128)(2,1)}, u32[]{:S(2)}) copy-start(bf16[64,64]{1,0:T(8,128)(2,1)} %param.18) | copy-start | bytes 24580
  8.0 6.7 %copy-start.11 = (s32[1024]{0:T(1024)S(1)}, s32[1024]{0:T(1024)}, u32[]{:S(2)}) copy-start(s32[1024]{0:T(1024)} %param.11) | copy-start | bytes 12292
  13.1 6.6 %collective-permute-start = (bf16[2,16,4,512,16]{3,4,1,2,0:T(8,128)(2,1)S(1)}, bf16[2,16,4,512,16]{3,4,1,2,0:T(8,128)(2,1)}, u32[]{:S(2)}, u32[]{:S(2)}) collective-permute-start(bf16[2,16,4,512,16]{3,4,1,2,0:T(8,128)(2,1)S(1)} %convert_bitcast_fusion.2), channel_id=1, source_target_pairs={{0,1},{1,0},{2,3},{3,2},{4,5},{5,4},{6,7},{7,6},{8,9},{9,8},{10,11... | collective-permute-start | bytes 6291464 | tf_op jit(solution)/shard_map/while/body/eval_jaxpr/ppermute | solution.py:77
  103.3 3.2 %copy-start.3 = (bf16[16,4,512,16]{2,3,1,0:T(8,128)(2,1)S(1)}, bf16[16,4,512,16]{2,3,1,0:T(8,128)(2,1)}, u32[]{:S(2)}) copy-start(bf16[16,4,512,16]{2,3,1,0:T(8,128)(2,1)} %fusion.20) | copy-start | bytes 3145732
  103.3 3.2 %copy-start.5 = (bf16[16,4,512,16]{2,3,0,1:T(8,128)(2,1)S(1)}, bf16[16,4,512,16]{2,3,0,1:T(8,128)(2,1)}, u32[]{:S(2)}) copy-start(bf16[16,4,512,16]{2,3,0,1:T(8,128)(2,1)} %get-tuple-element.28) | copy-start | bytes 3145732
  106.5 24.8 %copy-start.2 = (f32[4,512,512]{1,2,0:T(8,128)}, f32[4,512,512]{1,2,0:T(8,128)S(1)}, u32[]{:S(2)}) copy-start(f32[4,512,512]{1,2,0:T(8,128)S(1)} %get-tuple-element.26) | copy-start | bytes 12582916
  106.5 75.4 %copy-start.1 = (f32[4,512,512]{1,2,0:T(8,128)}, f32[4,512,512]{1,2,0:T(8,128)S(1)}, u32[]{:S(2)}) copy-start(f32[4,512,512]{1,2,0:T(8,128)S(1)} %get-tuple-element.25) | copy-start | bytes 12582916
  106.5 24.8 %copy-start.4 = (bf16[16,4,512,16]{2,3,0,1:T(8,128)(2,1)S(1)}, bf16[16,4,512,16]{2,3,0,1:T(8,128)(2,1)}, u32[]{:S(2)}) copy-start(bf16[16,4,512,16]{2,3,0,1:T(8,128)(2,1)} %get-tuple-element.40) | copy-start | bytes 3145732
  131.3 24.4 %copy-start.6 = (bf16[16,4,512,16]{2,3,0,1:T(8,128)(2,1)S(1)}, bf16[16,4,512,16]{2,3,0,1:T(8,128)(2,1)}, u32[]{:S(2)}) copy-start(bf16[16,4,512,16]{2,3,0,1:T(8,128)(2,1)} %get-tuple-element.29) | copy-start | bytes 3145732
Sparse Core Ops, SparseCore 0:
  12.4 69.5 all-gather.1
where the time goes:
time: 263 us
  matrix products  109 us (41%)
  waiting for transfers between devices  59.2 us (23%)
  other arithmetic  53.5 us (20%)
  blocking collectives  13.9 us (5%)
  between operations  13.7 us (5%)
  local copies, waits for them, and re-layouts  12.6 us (5%)
    all_gather x1, waiting for transfers between devices, bias_strip(): full_cols = lax.all_gather(bias_tile, 'col', axis=1, tiled=True)  59.2 us
    dot_general x2, matrix products, attend_block(): jnp.einsum('jhid,jhkd->jhik', query, kv_blk[0], preferred_element_type=jn...  49.1 us
    reduce_sum x1, other arithmetic, attend_block(): run_sum = run_sum * rescale + jnp.sum(p_exp, axis=-1)  45.5 us
    dot_general x1, matrix products, finish(): jnp.einsum('jhid,hdc->ijc', gated, w_o.reshape(heads, head_dim, w_o.shape...  28.5 us
    dot_general x1, matrix products, attend_block(): jnp.einsum('jhik,jhkd->jhid', p_exp.astype(jnp.bfloat16), kv_blk[1], pref...  26.2 us
    all_to_all x1, blocking collectives, bias_strip(): own_rows = lax.all_to_all(full_cols, 'row', 1, 0, tiled=True)  13.9 us
    all_to_all x1, local copies, waits for them, and re-layouts, bias_strip(): own_rows = lax.all_to_all(full_cols, 'row', 1, 0, tiled=True)  7.45 us
  transfers between devices with their start and end apart: 2, of which 1 were waited for; matrix products, arithmetic and copies ran while one was open for 3% of the time, Pallas kernels for 0%

commit v1 on v0

v1 whole, which is shorter than its diff:
```python
import functools
import math
import jax
import jax.numpy as jnp
from jax import lax
from jax.experimental import pallas as pl
from jax.experimental.pallas import tpu as pltpu
from jax.sharding import PartitionSpec as P

LN_EPS = 1e-5
LOG2E = math.log2(math.e)
FILL_PARTS = (-998244352.0, -1753088.0, -2560.0)
J, C, R, H, D = 16, 64, 512, 4, 16
NIB = 4
MESH = pl.DeviceIdType.MESH
BF, F32 = jnp.bfloat16, jnp.float32
PARTS = ((0, 3), (3, 3), (6, 2))
ORDERS = (("x", "y", "z"), ("y", "z", "x"), ("z", "x", "y"))
GROUPS = 2


class Gather:
    def __init__(self, bias_all, send_sem, recv_sem):
        self.buf, self.send_sem, self.recv_sem = bias_all, send_sem, recv_sem
        self.col, self.row = lax.axis_index("col"), lax.axis_index("row")
        self.z, self.y, self.x = self.col // 16, (self.col // 4) % 4, self.col % 4
        self.turn = (self.z - 2 * self.row + 4) % 4
        self.source = self.turn < 2

    def neighbour(self, dim, step):
        z, y, x = self.z, self.y, self.x
        if dim == "z":
            z = (z + step + 4) % 4
        elif dim == "y":
            y = (y + step + 4) % 4
        else:
            x = (x + step + 4) % 4
        return {"col": (z * 4 + y) * 4 + x, "row": self.row}

    def view(self, group, part, phase, value, head):
        order = ORDERS[part]
        pos = {}
        for n, dim in enumerate(order):
            if n < phase:
                pos[dim] = slice(None)
            elif n == phase:
                pos[dim] = value
            else:
                pos[dim] = {"z": self.z % 2, "y": self.y, "x": self.x}[dim]
        lo, size = PARTS[part]
        first = group * 2 if head is None else group * 2 + head
        return self.buf.at[pl.ds(first, 2 if head is None else 1), pl.ds(lo, size), pos["z"], pos["y"], pos["x"]]

    def copy(self, group, part, phase, slot, value, head, step):
        dim = ORDERS[part][phase]
        sem = ((group * 3 + part) * 3 + phase) * 4 + slot
        ref = self.view(group, part, phase, value, head)
        return pltpu.make_async_remote_copy(src_ref=ref, dst_ref=ref, send_sem=self.send_sem.at[sem], recv_sem=self.recv_sem.at[sem], device_id=self.neighbour(dim, step), device_id_type=MESH)

    def here(self, dim):
        return {"z": self.z % 2, "y": self.y, "x": self.x}[dim]

    def first(self, group, part, phase, act):
        order = ORDERS[part]
        dim = order[phase]

        def go():
            for slot, step in ((0, 1), (1, -1)):
                getattr(self.copy(group, part, phase, slot, self.here(dim), None, step), act)()

        if "z" in order[phase:]:
            pl.when(self.source)(go)
        else:
            go()

    def relay(self, group, part, phase, act):
        order = ORDERS[part]
        dim = order[phase]
        if dim == "z":
            cases = ((0, 1, 1, 0, -1, 3), (1, 0, 0, 0, 1, 2), (2, 0, 1, 1, 1, 2), (3, 1, 0, 1, -1, 3))
            for turn, slot, value, head, step, out in cases:

                @pl.when(self.turn == turn)
                def _():
                    if act == "start":
                        self.copy(group, part, phase, slot, value, None, 1).wait_recv()
                    getattr(self.copy(group, part, phase, out, value, head, step), act)()

            return

        def go():
            here = self.here(dim)
            behind, ahead = (here + 3) % 4, (here + 1) % 4
            if act == "start":
                self.copy(group, part, phase, 0, behind, None, 1).wait_recv()
            getattr(self.copy(group, part, phase, 2, behind, 0, 1), act)()
            if act == "start":
                self.copy(group, part, phase, 1, ahead, None, -1).wait_recv()
            getattr(self.copy(group, part, phase, 3, ahead, 1, -1), act)()

        if "z" in order[phase:]:
            pl.when(self.source)(go)
        else:
            go()

    def finish(self, group, part, phase):
        order = ORDERS[part]
        dim = order[phase]
        if dim == "z":
            for turn, value, slots in ((2, 0, ((2, 0), (3, 1))), (3, 1, ((3, 0), (2, 1)))):

                @pl.when(self.turn == turn)
                def _():
                    for slot, head in slots:
                        self.copy(group, part, phase, slot, value, head, 1).wait_recv()

            return

        def go():
            far = (self.here(dim) + 2) % 4
            self.copy(group, part, phase, 2, far, 0, 1).wait_recv()
            self.copy(group, part, phase, 3, far, 1, -1).wait_recv()

        if "z" in order[phase:]:
            pl.when(self.source)(go)
        else:
            go()

    def everywhere(self, method, phase, *extra, groups=range(GROUPS)):
        for group in groups:
            for part in range(3):
                method(group, part, phase, *extra)


def kernel(pair_ref, mask_ref, gamma_ref, beta_ref, wt_ref, wbt_ref, wot_ref, out_ref,
           normed, bias_f32, bias_own, bias_all, query, keys_t, keys, values, gate, gated, const, fill_rows, bias_kt, logits,
           send_sem, recv_sem, own_send, own_recv, kv_send, kv_recv):
    row = lax.axis_index("row")
    gather = Gather(bias_all, send_sem, recv_sem)
    owner = gather.z // 2
    partner = {"row": 1 - row}

    barrier = pltpu.get_barrier_semaphore()
    peers = [partner] + [gather.neighbour(dim, step) for dim in "xyz" for step in (1, -1)]
    for peer in peers:
        pl.semaphore_signal(barrier, inc=1, device_id=peer, device_id_type=MESH)

    gamma, beta = gamma_ref[...], beta_ref[...]
    wbt = wbt_ref[...]
    for j in range(J):
        pair = pair_ref[j].astype(F32)
        mean = jnp.mean(pair, axis=0, keepdims=True)
        centred = pair - mean
        variance = jnp.mean(centred * centred, axis=0, keepdims=True)
        a = (centred * lax.rsqrt(variance + LN_EPS) * gamma + beta).astype(BF)
        normed[j] = a
        b = jnp.dot(wbt, a, preferred_element_type=F32)
        for h in range(H):
            bias_f32[h, j:j + 1, :] = b[h:h + 1, :]
    for h in range(H):
        for t in range(4):
            bias_own[h, t] = bias_f32[h, :, t * 128:(t + 1) * 128].astype(BF)

    pl.semaphore_wait(barrier, len(peers))

    def own_place(r):
        return bias_all.at[:, pl.ds(r * 4, 4), gather.z % 2, gather.y, gather.x]

    def own_away():
        return pltpu.make_async_remote_copy(src_ref=bias_own, dst_ref=own_place(row), send_sem=own_send.at[0], recv_sem=own_recv.at[0], device_id=partner, device_id_type=MESH)

    def own_stay():
        return pltpu.make_async_copy(bias_own, own_place(row), own_send.at[1])

    @pl.when(row != owner)
    def _():
        own_away().start()

    @pl.when(row == owner)
    def _():
        own_stay().start()
        own_stay().wait()
        pltpu.make_async_remote_copy(src_ref=bias_own, dst_ref=own_place(1 - row), send_sem=own_send.at[0], recv_sem=own_recv.at[0], device_id=partner, device_id_type=MESH).wait_recv()

    gather.everywhere(gather.first, 0, "start")

    rows_i = lax.broadcasted_iota(jnp.int32, (64, 256), 0)
    const[0:64, :] = jnp.where(rows_i < 3, 1.0, 0.0).astype(BF)
    eye_r = lax.broadcasted_iota(jnp.int32, (128, 256), 0)
    eye_c = lax.broadcasted_iota(jnp.int32, (128, 256), 1)
    const[64:192, :] = jnp.where((eye_c == eye_r) | (eye_c == eye_r + 128), 1.0, 0.0).astype(BF)
    shut = jnp.where(mask_ref[pl.ds(row, 1), :] > 0, 0.0, 1.0)
    piece = lax.broadcasted_iota(jnp.int32, (64, R), 0)
    fill = jnp.where(piece == 0, FILL_PARTS[0], jnp.where(piece == 1, FILL_PARTS[1], jnp.where(piece == 2, FILL_PARTS[2], 0.0)))
    fill_rows[...] = (fill * shut).astype(BF)

    wt = wt_ref[...]

    def project(j, carry):
        r = jnp.dot(wt, normed[j], preferred_element_type=F32)
        q = (r[0:64] * (1.0 / math.sqrt(D))).astype(BF)
        k = r[64:128].astype(BF)
        v = r[128:192].astype(BF)
        g = jax.nn.sigmoid(r[192:256])
        for h in range(H):
            sl = slice(h * D, (h + 1) * D)
            keys_t[h, j] = k[sl]
            values[row, h, j] = v[sl]
            for ib in range(NIB):
                query[h, ib, j] = q[sl, ib * 128:(ib + 1) * 128]
                gate[h, ib, j] = g[sl, ib * 128:(ib + 1) * 128]
        return carry

    lax.fori_loop(0, 8, project, 0)
    gather.everywhere(gather.relay, 0, "start")
    lax.fori_loop(8, 16, project, 0)
    gather.everywhere(gather.finish, 0)
    gather.everywhere(gather.first, 1, "start")

    def turn_keys(n, carry):
        kt = keys_t[n // 4, pl.ds((n % 4) * 4, 4)].reshape(64, R)
        full = jnp.concatenate([kt, fill_rows[...]], axis=0)
        keys[row, n] = full.T
        return carry

    lax.fori_loop(0, 16, turn_keys, 0)

    def kv_copy(which):
        ref = (keys if which == 0 else values).at[row]
        return pltpu.make_async_remote_copy(src_ref=ref, dst_ref=ref, send_sem=kv_send.at[which], recv_sem=kv_recv.at[which], device_id=partner, device_id_type=MESH)

    kv_copy(1).start()
    gather.everywhere(gather.relay, 1, "start")
    kv_copy(0).start()
    gather.everywhere(gather.finish, 1)
    gather.everywhere(gather.first, 2, "start")
    for which in (0, 1):
        ref = (keys if which == 0 else values).at[1 - row]
        pltpu.make_async_remote_copy(src_ref=ref, dst_ref=ref, send_sem=kv_send.at[which], recv_sem=kv_recv.at[which], device_id=partner, device_id_type=MESH).wait_recv()
    gather.everywhere(gather.relay, 2, "start", groups=(0,))
    gather.everywhere(gather.finish, 2, groups=(0,))

    attend_heads(0, bias_all, query, keys, values, gate, gated, const, bias_kt, logits,
                 after_first=lambda: gather.everywhere(gather.relay, 2, "start", groups=(1,)))
    gather.everywhere(gather.finish, 2, groups=(1,))
    attend_heads(2, bias_all, query, keys, values, gate, gated, const, bias_kt, logits)
    project_out(pair_ref, wot_ref, gated, out_ref)

    for phase in range(3):
        gather.everywhere(gather.first, phase, "wait_send")
        gather.everywhere(gather.relay, phase, "wait_send")
    kv_copy(0).wait_send()
    kv_copy(1).wait_send()

    @pl.when(row != owner)
    def _():
        own_away().wait_send()


def attend_heads(head_lo, bias_all, query, keys, values, gate, gated, const, bias_kt, logits, after_first=None):
    def unit(n):
        h, ib = head_lo + n // NIB, n % NIB
        for t in range(8):
            block = bias_all[h, t, ib // 2, pl.ds((ib % 2) * 2, 2)].reshape(128, 128)
            bias_kt[t * 128:(t + 1) * 128, :] = block.T

        def score(p):
            group, odd = p // 2, p % 2
            zero = jnp.zeros((16, 128), BF)
            gap = jnp.zeros((16, 256), BF)
            left = jnp.concatenate([query[h, ib, 2 * p], zero], axis=1)
            right = jnp.concatenate([zero, query[h, ib, 2 * p + 1]], axis=1)
            top = [gap, gap, left, right] if odd else [left, right, gap, gap]
            rhs = jnp.concatenate(top + [const[...]], axis=0)
            best = None
            for kh in range(2):
                lhs = jnp.concatenate([keys[kh, h * 4 + group], bias_kt[kh * R:(kh + 1) * R, :]], axis=1)
                s = jnp.dot(lhs, rhs, preferred_element_type=F32)
                logits[p % 2, kh * R:(kh + 1) * R, :] = s
                m = jnp.max(s, axis=0, keepdims=True)
                best = m if best is None else jnp.maximum(best, m)
            return best

        def mix(p, best):
            total = jnp.zeros((1, 256), F32)
            acc = None
            for kh in range(2):
                e = jnp.exp2((logits[p % 2, kh * R:(kh + 1) * R, :] - best) * LOG2E)
                total = total + jnp.sum(e, axis=0, keepdims=True)
                v = jnp.concatenate([values[kh, h, 2 * p], values[kh, h, 2 * p + 1]], axis=0)
                o = jnp.dot(v, e.astype(BF), preferred_element_type=F32)
                acc = o if acc is None else acc + o
            scale = 1.0 / total
            gated[ib, 2 * p, h] = (gate[h, ib, 2 * p] * (acc[0:16, 0:128] * scale[:, 0:128])).astype(BF)
            gated[ib, 2 * p + 1, h] = (gate[h, ib, 2 * p + 1] * (acc[16:32, 128:256] * scale[:, 128:256])).astype(BF)

        best = score(0)
        for p in range(8):
            later = score(p + 1) if p < 7 else None
            mix(p, best)
            best = later

    if after_first is None:
        pl.loop(0, 2 * NIB)(unit)
    else:
        pl.loop(0, 1)(unit)
        after_first()
        pl.loop(1, 2 * NIB)(unit)


def project_out(pair_ref, wot_ref, gated, out_ref):
    wot = wot_ref[...]

    def one(j, carry):
        g = jnp.concatenate([gated[ib, j].reshape(64, 128) for ib in range(NIB)], axis=1)
        update = jnp.dot(wot, g, preferred_element_type=F32)
        out_ref[j] = (pair_ref[j].astype(F32) + update).astype(BF)
        return carry

    lax.fori_loop(0, J, one, 0)


SCRATCH = dict(
    normed=((J, C, R), BF), bias_f32=((H, J, R), F32), bias_own=((H, 4, J, 128), BF), bias_all=((H, 8, 2, 4, 4, J, 128), BF),
    query=((H, NIB, J, D, 128), BF), keys_t=((H, J, D, R), BF), keys=((2, 16, R, 128), BF), values=((2, H, J, D, R), BF),
    gate=((H, NIB, J, D, 128), F32), gated=((NIB, J, H, D, 128), BF), const=((192, 256), BF), fill_rows=((64, R), BF),
    bias_kt=((2 * R, 128), BF), logits=((2, 2 * R, 256), F32))


def solution(mesh):
    def body(pair_tile, res_mask, ln_gamma, ln_beta, w_q, w_k, w_v, w_b, w_g, w_o):
        pair_t = jnp.transpose(pair_tile, (1, 2, 0))
        wt = jnp.concatenate([w_q, w_k, w_v, w_g], axis=1).T
        wbt = jnp.pad(w_b.T, ((0, 4), (0, 0)))
        scratch = [pltpu.VMEM(shape, dtype) for shape, dtype in SCRATCH.values()]
        sems = [pltpu.SemaphoreType.DMA((GROUPS * 36,)), pltpu.SemaphoreType.DMA((GROUPS * 36,)), pltpu.SemaphoreType.DMA((2,)), pltpu.SemaphoreType.DMA((2,)), pltpu.SemaphoreType.DMA((2,)), pltpu.SemaphoreType.DMA((2,))]
        out_t = pl.pallas_call(
            kernel,
            out_shape=jax.ShapeDtypeStruct((J, C, R), BF),
            in_specs=[pl.BlockSpec(memory_space=pltpu.VMEM)] * 7,
            out_specs=pl.BlockSpec(memory_space=pltpu.VMEM),
            scratch_shapes=scratch + sems,
            compiler_params=pltpu.CompilerParams(collective_id=0, has_side_effects=True, vmem_limit_bytes=60 * 1024 * 1024),
        )(pair_t, res_mask.reshape(2, R), ln_gamma.reshape(C, 1), ln_beta.reshape(C, 1), wt, wbt, w_o.T)
        return jnp.transpose(out_t, (2, 0, 1))

    tile_spec = P(("data", "row"), "col", None)
    return jax.shard_map(body, mesh=mesh, in_specs=(tile_spec, P("data"), P(), P(), P(), P(), P(), P(), P(), P()), out_specs=tile_spec, check_vma=False)
```

time: 263 us -> 89.3 us (0.34)
  the two profiles are of different devices: /device:TPU:1 before, /device:TPU:0 now
where the time goes in v1:
time: 89.3 us; the launch traced here: 88.8 us
  Pallas kernels  78.1 us (87%)
  local copies, waits for them, and re-layouts  9.94 us (11%)
    pallas_call x1, Pallas kernels, body(): pl.pallas_call(kernel, out_shape=jax.ShapeDtypeStruct((J, C, R), BF), in_...  78.1 us
    unnamed x20, local copies, waits for them, and re-layouts  5.96 us

profile of v1, /device:TPU:0, one launch (start us, length us, event | category | flops | bytes accessed | tf_op | source)
XLA Modules:
  0.0 88.8 jit_solution(2162529938360510798)
XLA Ops:
  0.0 0.0 copy-start
  0.0 1.3 %pad.4.wbt_ref = bf16[8,64]{1,0:T(8,128)(2,1)} pad(bf16[4,64]{1,0:T(4,128)(2,1)} %bitcast.11, bf16[]{:T(256)} %constant.2.clone.1), padding=0_4x0_0 | pad | bytes 1538 | tf_op jit(solution)/shard_map/jit(_pad)/pad | solution.py:334
  1.3 1.3 %reshape.9.mask_ref = s32[2,512]{1,0:T(2,128)} reshape(s32[1024]{0:T(1024)} %param.11) | data formatting | bytes 8192 | tf_op jit(solution)/shard_map/reshape | solution.py:344
  2.6 0.0 copy-done
  2.6 0.0 copy-start.1
  2.6 0.1 copy.11
  2.7 0.6 copy-done.1
  3.3 0.0 copy-start.2
  3.3 0.1 copy.12
  3.4 0.6 copy-done.2
  4.0 0.0 copy-start.3
  4.0 0.1 copy.13
  4.1 0.6 copy-done.3
  4.7 0.1 copy.14
  4.8 0.0 copy-start.4
  4.8 0.6 maximum_bitcast_fusion.wt_ref
  5.5 0.1 copy-done.4
  5.5 0.7 copy.15
  6.2 0.0 copy-start.5
  6.2 0.7 copy-done.5
  6.9 0.0 copy-start.6
  6.9 0.7 copy.16.gamma_ref
  7.6 0.0 copy-done.6
  7.6 0.7 copy.17.beta_ref
  8.3 78.1 %shard_map.100 = bf16[16,64,512]{2,1,0:T(8,128)(2,1)} custom-call(bf16[16,64,512]{2,1,0:T(8,128)(2,1)} %bitcast.9, s32[2,512]{1,0:T(2,128)} %reshape.9.mask_ref, f32[64,1]{1,0:T(8,128)} %copy.16.gamma_ref, f32[64,1]{1,0:T(8,128)} %copy.17.beta_ref, bf16[256,64]{1,0:T(8,128)(2,1)} %maximum_bitcast_fusion.wt_ref, bf16[8,64]{1,0:T(8,128)(2,1)} %pad.4.wbt_ref, ...), custom_call_target="tpu_custom_call" | custom-call | tf_op jit(solution)/shard_map/pallas_call | solution.py:337
  86.5 2.3 %copy.19 = bf16[512,16,64]{0,2,1:T(8,128)(2,1)} copy(bf16[512,16,64]{0,2,1:T(8,128)(2,1)} %bitcast.8) | data formatting | bytes 2097152
Async XLA Ops:
  0.0 2.6 %copy-start = (bf16[64,64]{1,0:T(8,128)(2,1)S(1)}, bf16[64,64]{1,0:T(8,128)(2,1)}, u32[]{:S(2)}) copy-start(bf16[64,64]{1,0:T(8,128)(2,1)} %param.14) | copy-start | bytes 24580
  2.6 0.7 copy-start.1
  3.3 0.7 copy-start.2
  4.0 0.7 copy-start.3
  4.8 0.7 copy-start.4
  6.2 0.7 copy-start.5
  6.9 0.7 copy-start.6

commit v2 on v1

v2 whole, which is shorter than its diff:
```python
import functools
import math
import jax
import jax.numpy as jnp
from jax import lax
from jax.experimental import pallas as pl
from jax.experimental.pallas import tpu as pltpu
from jax.sharding import PartitionSpec as P

LN_EPS = 1e-5
LOG2E = math.log2(math.e)
FILL_PARTS = (-998244352.0, -1753088.0, -2560.0)
J, C, R, H, D = 16, 64, 512, 4, 16
NIB = 4
MESH = pl.DeviceIdType.MESH
BF, F32 = jnp.bfloat16, jnp.float32
PARTS = ((0, 3), (3, 3), (6, 2))
ORDERS = (("x", "y", "z"), ("y", "z", "x"), ("z", "x", "y"))


class Gather:
    def __init__(self, bias_all, send_sem, recv_sem):
        self.buf, self.send_sem, self.recv_sem = bias_all, send_sem, recv_sem
        self.col, self.row = lax.axis_index("col"), lax.axis_index("row")
        self.z, self.y, self.x = self.col // 16, (self.col // 4) % 4, self.col % 4
        self.turn = (self.z - 2 * self.row + 4) % 4
        self.source = self.turn < 2

    def neighbour(self, dim, step):
        z, y, x = self.z, self.y, self.x
        if dim == "z":
            z = (z + step + 4) % 4
        elif dim == "y":
            y = (y + step + 4) % 4
        else:
            x = (x + step + 4) % 4
        return {"col": (z * 4 + y) * 4 + x, "row": self.row}

    def here(self, dim):
        return {"z": self.z % 2, "y": self.y, "x": self.x}[dim]

    def copy(self, head, part, phase, slot, value, half, step):
        order = ORDERS[part]
        pos = {}
        for n, dim in enumerate(order):
            pos[dim] = slice(None) if n < phase else value if n == phase else self.here(dim)
        if half is not None:
            dim, size = ("y", 2) if part == 0 else ("z", 1)
            pos[dim] = pl.ds(half * size, size)
        lo, size = PARTS[part]
        ref = self.buf.at[head, pl.ds(lo, size), pos["z"], pos["y"], pos["x"]]
        sem = ((head * 3 + part) * 3 + phase) * 4 + slot
        return pltpu.make_async_remote_copy(src_ref=ref, dst_ref=ref, send_sem=self.send_sem.at[sem], recv_sem=self.recv_sem.at[sem], device_id=self.neighbour(order[phase], step), device_id_type=MESH)

    def among(self, part, phase, go):
        pl.when(self.source)(go) if "z" in ORDERS[part][phase:] else go()

    def first(self, head, phase, act="start"):
        for part in range(3):

            def go():
                for slot, step in ((0, 1), (1, -1), (2, 2))[: 2 if phase == 2 else 3]:
                    getattr(self.copy(head, part, phase, slot, self.here(ORDERS[part][phase]), None, step), act)()

            self.among(part, phase, go)

    def arrived(self, head, phase):
        for part in range(3):
            dim = ORDERS[part][phase]
            if dim == "z":
                for turn, waits in enumerate((((1, 1),), ((0, 0),), ((0, 1), (2, 0)), ((1, 0), (2, 1)))):

                    @pl.when(self.turn == turn)
                    def _():
                        for slot, value in waits:
                            self.copy(head, part, phase, slot, value, None, 1).wait_recv()

                continue

            def go():
                for slot, back in ((0, 3), (1, 1), (2, 2)):
                    self.copy(head, part, phase, slot, (self.here(dim) + back) % 4, None, 1).wait_recv()

            self.among(part, phase, go)

    def relay(self, head, act="start"):
        for part in range(3):
            dim = ORDERS[part][2]
            if dim == "z":
                cases = ((0, 1, 1, 0, -1, 3), (1, 0, 0, 0, 1, 2), (2, 0, 1, 1, 1, 2), (3, 1, 0, 1, -1, 3))
                for turn, slot, value, half, step, out in cases:

                    @pl.when(self.turn == turn)
                    def _():
                        if act == "start":
                            self.copy(head, part, 2, slot, value, None, 1).wait_recv()
                        getattr(self.copy(head, part, 2, out, value, half, step), act)()

                continue
            for slot, back, half, step in ((0, 3, 0, 1), (1, 1, 1, -1)):
                value = (self.here(dim) + back) % 4
                if act == "start":
                    self.copy(head, part, 2, slot, value, None, 1).wait_recv()
                getattr(self.copy(head, part, 2, slot + 2, value, half, step), act)()

    def finish(self, head):
        for part in range(3):
            dim = ORDERS[part][2]
            if dim == "z":
                for turn, value, slots in ((2, 0, ((2, 0), (3, 1))), (3, 1, ((3, 0), (2, 1)))):

                    @pl.when(self.turn == turn)
                    def _():
                        for slot, half in slots:
                            self.copy(head, part, 2, slot, value, half, 1).wait_recv()

                continue
            for slot, half in ((2, 0), (3, 1)):
                self.copy(head, part, 2, slot, (self.here(dim) + 2) % 4, half, 1).wait_recv()

    def step1(self, head):
        self.arrived(head, 0)
        self.first(head, 1)

    def step2(self, head):
        self.arrived(head, 1)
        self.first(head, 2)


def kernel(pair_ref, mask_ref, gamma_ref, beta_ref, wq_ref, wk_ref, wv_ref, wg_ref, wbt_ref, wo_ref, out_ref,
           normed, bias_f32, bias_own, bias_all, query, keys_t, keys, values, gate, gated, const, fill_rows, weights, bias_kt, logits,
           send_sem, recv_sem, own_send, own_recv, kv_send, kv_recv):
    row = lax.axis_index("row")
    gather = Gather(bias_all, send_sem, recv_sem)
    owner = gather.z // 2
    partner = {"row": 1 - row}

    barrier = pltpu.get_barrier_semaphore()
    peers = [partner] + [gather.neighbour(dim, step) for dim in "xyz" for step in (1, -1, 2)]
    for peer in peers:
        pl.semaphore_signal(barrier, inc=1, device_id=peer, device_id_type=MESH)

    diag = lax.broadcasted_iota(jnp.int32, (C, C), 0) == lax.broadcasted_iota(jnp.int32, (C, C), 1)
    gamma = jnp.sum(jnp.where(diag, gamma_ref[...], 0.0), axis=1, keepdims=True)
    beta = jnp.sum(jnp.where(diag, beta_ref[...], 0.0), axis=1, keepdims=True)
    wbt = wbt_ref[...]
    for j in range(J):
        pair = pair_ref[j].astype(F32)
        mean = jnp.mean(pair, axis=0, keepdims=True)
        centred = pair - mean
        variance = jnp.mean(centred * centred, axis=0, keepdims=True)
        a = (centred * lax.rsqrt(variance + LN_EPS) * gamma + beta).astype(BF)
        normed[j] = a
        b = jnp.dot(wbt, a, preferred_element_type=F32)
        for h in range(H):
            bias_f32[h, j:j + 1, :] = b[h:h + 1, :]
    for h in range(H):
        for t in range(4):
            bias_own[h, t] = bias_f32[h, :, t * 128:(t + 1) * 128].astype(BF)

    pl.semaphore_wait(barrier, len(peers))

    def own_place(r):
        return bias_all.at[:, pl.ds(r * 4, 4), gather.z % 2, gather.y, gather.x]

    def own_away():
        return pltpu.make_async_remote_copy(src_ref=bias_own, dst_ref=own_place(row), send_sem=own_send.at[0], recv_sem=own_recv.at[0], device_id=partner, device_id_type=MESH)

    def own_stay():
        return pltpu.make_async_copy(bias_own, own_place(row), own_send.at[1])

    @pl.when(row != owner)
    def _():
        own_away().start()

    @pl.when(row == owner)
    def _():
        own_stay().start()
        own_stay().wait()
        pltpu.make_async_remote_copy(src_ref=bias_own, dst_ref=own_place(1 - row), send_sem=own_send.at[0], recv_sem=own_recv.at[0], device_id=partner, device_id_type=MESH).wait_recv()

    for h in range(H):
        gather.first(h, 0)

    rows_i = lax.broadcasted_iota(jnp.int32, (64, 256), 0)
    const[0:64, :] = jnp.where(rows_i < 3, 1.0, 0.0).astype(BF)
    eye_r = lax.broadcasted_iota(jnp.int32, (128, 256), 0)
    eye_c = lax.broadcasted_iota(jnp.int32, (128, 256), 1)
    const[64:192, :] = jnp.where((eye_c == eye_r) | (eye_c == eye_r + 128), 1.0, 0.0).astype(BF)
    piece = lax.broadcasted_iota(jnp.int32, (64, 128), 0)
    fill = jnp.where(piece == 0, FILL_PARTS[0], jnp.where(piece == 1, FILL_PARTS[1], jnp.where(piece == 2, FILL_PARTS[2], 0.0)))
    for t in range(4):
        shut = jnp.where(mask_ref[pl.ds(row * 4 + t, 1), :] > 0, 0.0, 1.0)
        fill_rows[:, t * 128:(t + 1) * 128] = (fill * shut).astype(BF)
    for n, w_ref in enumerate((wq_ref, wk_ref, wv_ref, wg_ref, wo_ref)):
        weights[n * C:(n + 1) * C, :] = w_ref[...].T
    wt = weights[0:4 * C, :]

    def project(j, carry):
        r = jnp.dot(wt, normed[j], preferred_element_type=F32)
        q = (r[0:64] * (1.0 / math.sqrt(D))).astype(BF)
        k = r[64:128].astype(BF)
        v = r[128:192].astype(BF)
        g = jax.nn.sigmoid(r[192:256])
        for h in range(H):
            sl = slice(h * D, (h + 1) * D)
            keys_t[h, j] = k[sl]
            values[row, h, j] = v[sl]
            for ib in range(NIB):
                query[h, ib, j] = q[sl, ib * 128:(ib + 1) * 128]
                gate[h, ib, j] = g[sl, ib * 128:(ib + 1) * 128]
        return carry

    def turn_keys(n, carry):
        kt = keys_t[n // 4, pl.ds((n % 4) * 4, 4)].reshape(64, R)
        full = jnp.concatenate([kt, fill_rows[...]], axis=0)
        keys[row, n] = full.T
        return carry

    def kv_copies(h, r):
        for n, ref in enumerate((keys.at[r, pl.ds(h * 4, 4)], values.at[r, h])):
            yield pltpu.make_async_remote_copy(src_ref=ref, dst_ref=ref, send_sem=kv_send.at[h * 2 + n], recv_sem=kv_recv.at[h * 2 + n], device_id=partner, device_id_type=MESH)

    lax.fori_loop(0, 8, project, 0)
    gather.step1(0)
    lax.fori_loop(8, 16, project, 0)
    gather.step2(0)
    gather.step1(1)
    lax.fori_loop(0, 16, turn_keys, 0)
    for h in range(H):
        for copy in kv_copies(h, row):
            copy.start()
    gather.relay(0)
    gather.step2(1)

    @pl.loop(0, H * NIB)
    def _(n):
        h, ib = n // NIB, n % NIB

        @pl.when(ib == 0)
        def _():
            for copy in kv_copies(h, 1 - row):
                copy.wait_recv()
            gather.finish(h)

        @pl.when((ib == 0) & (h < H - 2))
        def _():
            gather.step1(h + 2)

        @pl.when((ib == 1) & (h < H - 1))
        def _():
            gather.relay(h + 1)

        @pl.when((ib == 2) & (h < H - 2))
        def _():
            gather.step2(h + 2)

        attend(h, ib, bias_all, query, keys, values, gate, gated, const, bias_kt, logits)

    project_out(pair_ref, weights, gated, out_ref)

    @pl.loop(0, H)
    def _(h):
        for phase in range(3):
            gather.first(h, phase, "wait_send")
        gather.relay(h, "wait_send")
        for copy in kv_copies(h, row):
            copy.wait_send()

    @pl.when(row != owner)
    def _():
        own_away().wait_send()


def attend(h, ib, bias_all, query, keys, values, gate, gated, const, bias_kt, logits):
    for t in range(8):
        block = bias_all[h, t, ib // 2, pl.ds((ib % 2) * 2, 2)].reshape(128, 128)
        bias_kt[t * 128:(t + 1) * 128, :] = block.T

    def score(p):
        group, odd = p // 2, p % 2
        zero = jnp.zeros((16, 128), BF)
        gap = jnp.zeros((16, 256), BF)
        left = jnp.concatenate([query[h, ib, 2 * p], zero], axis=1)
        right = jnp.concatenate([zero, query[h, ib, 2 * p + 1]], axis=1)
        top = [gap, gap, left, right] if odd else [left, right, gap, gap]
        rhs = jnp.concatenate(top + [const[...]], axis=0)
        best = None
        for kh in range(2):
            lhs = jnp.concatenate([keys[kh, h * 4 + group], bias_kt[kh * R:(kh + 1) * R, :]], axis=1)
            s = jnp.dot(lhs, rhs, preferred_element_type=F32)
            logits[p % 2, kh * R:(kh + 1) * R, :] = s
            m = jnp.max(s, axis=0, keepdims=True)
            best = m if best is None else jnp.maximum(best, m)
        return best

    def mix(p, best):
        total = jnp.zeros((1, 256), F32)
        acc = None
        for kh in range(2):
            e = jnp.exp2((logits[p % 2, kh * R:(kh + 1) * R, :] - best) * LOG2E)
            total = total + jnp.sum(e, axis=0, keepdims=True)
            v = jnp.concatenate([values[kh, h, 2 * p], values[kh, h, 2 * p + 1]], axis=0)
            o = jnp.dot(v, e.astype(BF), preferred_element_type=F32)
            acc = o if acc is None else acc + o
        scale = 1.0 / total
        gated[ib, 2 * p, h] = (gate[h, ib, 2 * p] * (acc[0:16, 0:128] * scale[:, 0:128])).astype(BF)
        gated[ib, 2 * p + 1, h] = (gate[h, ib, 2 * p + 1] * (acc[16:32, 128:256] * scale[:, 128:256])).astype(BF)

    best = score(0)
    for p in range(8):
        later = score(p + 1) if p < 7 else None
        mix(p, best)
        best = later


def project_out(pair_ref, weights, gated, out_ref):
    wot = weights[4 * C:5 * C, :]

    def one(j, carry):
        g = jnp.concatenate([gated[ib, j].reshape(64, 128) for ib in range(NIB)], axis=1)
        update = jnp.dot(wot, g, preferred_element_type=F32)
        out_ref[j] = (pair_ref[j].astype(F32) + update).astype(BF)
        return carry

    lax.fori_loop(0, J, one, 0)


SCRATCH = dict(
    normed=((J, C, R), BF), bias_f32=((H, J, R), F32), bias_own=((H, 4, J, 128), BF), bias_all=((H, 8, 2, 4, 4, J, 128), BF),
    query=((H, NIB, J, D, 128), BF), keys_t=((H, J, D, R), BF), keys=((2, 16, R, 128), BF), values=((2, H, J, D, R), BF),
    gate=((H, NIB, J, D, 128), F32), gated=((NIB, J, H, D, 128), BF), const=((192, 256), BF), fill_rows=((64, R), BF), weights=((5 * C, C), BF),
    bias_kt=((2 * R, 128), BF), logits=((2, 2 * R, 256), F32))


def solution(mesh):
    def body(pair_tile, res_mask, ln_gamma, ln_beta, w_q, w_k, w_v, w_b, w_g, w_o):
        pair_t = jnp.transpose(pair_tile, (1, 2, 0))
        scratch = [pltpu.VMEM(shape, dtype) for shape, dtype in SCRATCH.values()]
        sems = [pltpu.SemaphoreType.DMA((n,)) for n in (H * 36, H * 36, 2, 1, 2 * H, 2 * H)]
        out_t = pl.pallas_call(
            kernel,
            out_shape=jax.ShapeDtypeStruct((J, C, R), BF),
            in_specs=[pl.BlockSpec(memory_space=pltpu.VMEM)] * 10,
            out_specs=pl.BlockSpec(memory_space=pltpu.VMEM),
            scratch_shapes=scratch + sems,
            compiler_params=pltpu.CompilerParams(collective_id=0, has_side_effects=True, vmem_limit_bytes=60 * 1024 * 1024),
        )(pair_t, res_mask.reshape(8, 128), ln_gamma.reshape(1, C), ln_beta.reshape(1, C), w_q, w_k, w_v, w_g, w_b.T, w_o)
        return jnp.transpose(out_t, (2, 0, 1))

    tile_spec = P(("data", "row"), "col", None)
    return jax.shard_map(body, mesh=mesh, in_specs=(tile_spec, P("data"), P(), P(), P(), P(), P(), P(), P(), P()), out_specs=tile_spec, check_vma=False)
```

time: 89.3 us -> 83.1 us (0.931)
  the two profiles are of different devices: /device:TPU:0 before, /device:TPU:1 now
where the time goes in v2:
time: 83.1 us; the launch traced here: 82.9 us
  Pallas kernels  80.6 us (97%)
  local copies, waits for them, and re-layouts  2.29 us (3%)
    pallas_call x1, Pallas kernels, body(): pl.pallas_call(kernel, out_shape=jax.ShapeDtypeStruct((J, C, R), BF), in_...  80.6 us
    unnamed x1, local copies, waits for them, and re-layouts  2.29 us

profile of v2, /device:TPU:1, one launch (start us, length us, event | category | flops | bytes accessed | tf_op | source)
XLA Modules:
  0.0 82.9 jit_solution(10839146688449752690)
XLA Ops:
  0.0 80.6 %shard_map.100 = bf16[16,64,512]{2,1,0:T(8,128)(2,1)} custom-call(bf16[16,64,512]{2,1,0:T(8,128)(2,1)} %bitcast.7, s32[8,128]{1,0:T(8,128)} %bitcast.8, f32[1,64]{1,0:T(1,128)} %bitcast.10, f32[1,64]{1,0:T(1,128)} %bitcast.11, bf16[64,64]{1,0:T(8,128)(2,1)} %wq_ref.1, bf16[64,64]{1,0:T(8,128)(2,1)} %wk_ref.1, bf16[64,64]{1,0:T(8,128)(2,1)} %wv_ref.1, ...), custom_call_target="tpu_custom_call" | custom-call | tf_op jit(solution)/shard_map/pallas_call | solution.py:341
  80.6 2.3 %copy.12 = bf16[512,16,64]{0,2,1:T(8,128)(2,1)} copy(bf16[512,16,64]{0,2,1:T(8,128)(2,1)} %bitcast.6) | data formatting | bytes 2097152

commit v3 on v2

--- a/solution.py
+++ b/solution.py
@@ -20,7 +20,7 @@
 
 class Gather:
     def __init__(self, bias_all, send_sem, recv_sem):
-        self.buf, self.send_sem, self.recv_sem = bias_all, send_sem, recv_sem
+        self.bufs, self.send_sem, self.recv_sem = bias_all, send_sem, recv_sem
         self.col, self.row = lax.axis_index("col"), lax.axis_index("row")
         self.z, self.y, self.x = self.col // 16, (self.col // 4) % 4, self.col % 4
         self.turn = (self.z - 2 * self.row + 4) % 4
@@ -45,10 +45,9 @@
         for n, dim in enumerate(order):
             pos[dim] = slice(None) if n < phase else value if n == phase else self.here(dim)
         if half is not None:
-            dim, size = ("y", 2) if part == 0 else ("z", 1)
-            pos[dim] = pl.ds(half * size, size)
-        lo, size = PARTS[part]
-        ref = self.buf.at[head, pl.ds(lo, size), pos["z"], pos["y"], pos["x"]]
+            size = 1 if order[1] == "z" else 2
+            pos[order[1]] = pl.ds(half * size, size)
+        ref = self.bufs[part].at[(head, pos[order[2]], pos[order[1]], pos[order[0]])]
         sem = ((head * 3 + part) * 3 + phase) * 4 + slot
         return pltpu.make_async_remote_copy(src_ref=ref, dst_ref=ref, send_sem=self.send_sem.at[sem], recv_sem=self.recv_sem.at[sem], device_id=self.neighbour(order[phase], step), device_id_type=MESH)
 
@@ -128,9 +127,10 @@
 
 
 def kernel(pair_ref, mask_ref, gamma_ref, beta_ref, wq_ref, wk_ref, wv_ref, wg_ref, wbt_ref, wo_ref, out_ref,
-           normed, bias_f32, bias_own, bias_all, query, keys_t, keys, values, gate, gated, const, fill_rows, weights, bias_kt, logits,
+           normed, bias_f32, bias_own, bias_a, bias_b, bias_c, query, keys_t, keys, values, gate, gated, const, fill_rows, weights, bias_kt, logits, best,
            send_sem, recv_sem, own_send, own_recv, kv_send, kv_recv):
     row = lax.axis_index("row")
+    bias_all = (bias_a, bias_b, bias_c)
     gather = Gather(bias_all, send_sem, recv_sem)
     owner = gather.z // 2
     partner = {"row": 1 - row}
@@ -160,24 +160,31 @@
 
     pl.semaphore_wait(barrier, len(peers))
 
-    def own_place(r):
-        return bias_all.at[:, pl.ds(r * 4, 4), gather.z % 2, gather.y, gather.x]
-
-    def own_away():
-        return pltpu.make_async_remote_copy(src_ref=bias_own, dst_ref=own_place(row), send_sem=own_send.at[0], recv_sem=own_recv.at[0], device_id=partner, device_id_type=MESH)
-
-    def own_stay():
-        return pltpu.make_async_copy(bias_own, own_place(row), own_send.at[1])
-
-    @pl.when(row != owner)
-    def _():
-        own_away().start()
-
-    @pl.when(row == owner)
-    def _():
-        own_stay().start()
-        own_stay().wait()
-        pltpu.make_async_remote_copy(src_ref=bias_own, dst_ref=own_place(1 - row), send_sem=own_send.at[0], recv_sem=own_recv.at[0], device_id=partner, device_id_type=MESH).wait_recv()
+    def own_copies(r):
+        for tiles, part, lo, size in (((0, 0, 0, 3), (3, 1, 0, 1)), ((0, 1, 1, 2), (2, 2, 0, 2)))[r]:
+            place = tuple(gather.here(dim) for dim in reversed(ORDERS[part]))
+            yield bias_own.at[:, pl.ds(tiles, size)], bias_all[part].at[(slice(None), *place, pl.ds(lo, size))]
+
+    def own_away(r):
+        for n, (src, dst) in enumerate(own_copies(r)):
+            yield pltpu.make_async_remote_copy(src_ref=src, dst_ref=dst, send_sem=own_send.at[n], recv_sem=own_recv.at[n], device_id=partner, device_id_type=MESH)
+
+    for r in range(2):
+
+        @pl.when((row == r) & (owner != r))
+        def _():
+            for copy in own_away(r):
+                copy.start()
+
+        @pl.when((row == r) & (owner == r))
+        def _():
+            stays = [pltpu.make_async_copy(src, dst, own_send.at[2 + n]) for n, (src, dst) in enumerate(own_copies(r))]
+            for copy in stays:
+                copy.start()
+            for copy in stays:
+                copy.wait()
+            for copy in own_away(1 - r):
+                copy.wait_recv()
 
     for h in range(H):
         gather.first(h, 0)
@@ -233,6 +240,9 @@
     gather.relay(0)
     gather.step2(1)
 
+    logits[1] = jnp.zeros((2 * R, 256), F32)
+    best[1] = jnp.zeros((1, 256), F32)
+
     @pl.loop(0, H * NIB)
     def _(n):
         h, ib = n // NIB, n % NIB
@@ -255,8 +265,10 @@
         def _():
             gather.step2(h + 2)
 
-        attend(h, ib, bias_all, query, keys, values, gate, gated, const, bias_kt, logits)
-
+        last = jnp.maximum(n - 1, 0)
+        attend(h, ib, (last // NIB, last % NIB), bias_all, query, keys, values, gate, gated, const, bias_kt, logits, best)
+
+    mix(7, H - 1, NIB - 1, values, gate, gated, logits, best)
     project_out(pair_ref, weights, gated, out_ref)
 
     @pl.loop(0, H)
@@ -267,15 +279,37 @@
         for copy in kv_copies(h, row):
             copy.wait_send()
 
-    @pl.when(row != owner)
-    def _():
-        own_away().wait_send()
-
-
-def attend(h, ib, bias_all, query, keys, values, gate, gated, const, bias_kt, logits):
+    for r in range(2):
+
+        @pl.when((row == r) & (owner != r))
+        def _():
+            for copy in own_away(r):
+                copy.wait_send()
+
+
+def mix(p, h, ib, values, gate, gated, logits, best):
+    total = jnp.zeros((1, 256), F32)
+    acc = None
+    for kh in range(2):
+        e = jnp.exp2((logits[p % 2, kh * R:(kh + 1) * R, :] - best[p % 2]) * LOG2E)
+        total = total + jnp.sum(e, axis=0, keepdims=True)
+        v = jnp.concatenate([values[kh, h, 2 * p], values[kh, h, 2 * p + 1]], axis=0)
+        o = jnp.dot(v, e.astype(BF), preferred_element_type=F32)
+        acc = o if acc is None else acc + o
+    scale = 1.0 / total
+    gated[ib, 2 * p, h] = (gate[h, ib, 2 * p] * (acc[0:16, 0:128] * scale[:, 0:128])).astype(BF)
+    gated[ib, 2 * p + 1, h] = (gate[h, ib, 2 * p + 1] * (acc[16:32, 128:256] * scale[:, 128:256])).astype(BF)
+
+
+def attend(h, ib, before, bias_all, query, keys, values, gate, gated, const, bias_kt, logits, best):
     for t in range(8):
-        block = bias_all[h, t, ib // 2, pl.ds((ib % 2) * 2, 2)].reshape(128, 128)
-        bias_kt[t * 128:(t + 1) * 128, :] = block.T
+        part = 0 if t < 3 else 1 if t < 6 else 2
+        z, y, tile = ib // 2, (ib % 2) * 2, t - PARTS[part][0]
+        rows = []
+        for n in range(8):
+            pos = {"z": z, "y": y + n // 4, "x": n % 4}
+            rows.append(bias_all[part][(h, *(pos[dim] for dim in reversed(ORDERS[part])), tile)])
+        bias_kt[t * 128:(t + 1) * 128, :] = jnp.concatenate(rows, axis=0).T
 
     def score(p):
         group, odd = p // 2, p % 2
@@ -285,33 +319,18 @@
         right = jnp.concatenate([zero, query[h, ib, 2 * p + 1]], axis=1)
         top = [gap, gap, left, right] if odd else [left, right, gap, gap]
         rhs = jnp.concatenate(top + [const[...]], axis=0)
-        best = None
+        high = None
         for kh in range(2):
             lhs = jnp.concatenate([keys[kh, h * 4 + group], bias_kt[kh * R:(kh + 1) * R, :]], axis=1)
             s = jnp.dot(lhs, rhs, preferred_element_type=F32)
             logits[p % 2, kh * R:(kh + 1) * R, :] = s
             m = jnp.max(s, axis=0, keepdims=True)
-            best = m if best is None else jnp.maximum(best, m)
-        return best
-
-    def mix(p, best):
-        total = jnp.zeros((1, 256), F32)
-        acc = None
-        for kh in range(2):
-            e = jnp.exp2((logits[p % 2, kh * R:(kh + 1) * R, :] - best) * LOG2E)
-            total = total + jnp.sum(e, axis=0, keepdims=True)
-            v = jnp.concatenate([values[kh, h, 2 * p], values[kh, h, 2 * p + 1]], axis=0)
-            o = jnp.dot(v, e.astype(BF), preferred_element_type=F32)
-            acc = o if acc is None else acc + o
-        scale = 1.0 / total
-        gated[ib, 2 * p, h] = (gate[h, ib, 2 * p] * (acc[0:16, 0:128] * scale[:, 0:128])).astype(BF)
-        gated[ib, 2 * p + 1, h] = (gate[h, ib, 2 * p + 1] * (acc[16:32, 128:256] * scale[:, 128:256])).astype(BF)
-
-    best = score(0)
+            high = m if high is None else jnp.maximum(high, m)
+        best[p % 2] = high
+
     for p in range(8):
-        later = score(p + 1) if p < 7 else None
-        mix(p, best)
-        best = later
+        score(p)
+        mix((p + 7) % 8, *((h, ib) if p else before), values, gate, gated, logits, best)
 
 
 def project_out(pair_ref, weights, gated, out_ref):
@@ -327,17 +346,17 @@
 
 
 SCRATCH = dict(
-    normed=((J, C, R), BF), bias_f32=((H, J, R), F32), bias_own=((H, 4, J, 128), BF), bias_all=((H, 8, 2, 4, 4, J, 128), BF),
+    normed=((J, C, R), BF), bias_f32=((H, J, R), F32), bias_own=((H, 4, J, 128), BF), bias_a=((H, 2, 4, 4, 3, J, 128), BF), bias_b=((H, 4, 2, 4, 3, J, 128), BF), bias_c=((H, 4, 4, 2, 2, J, 128), BF),
     query=((H, NIB, J, D, 128), BF), keys_t=((H, J, D, R), BF), keys=((2, 16, R, 128), BF), values=((2, H, J, D, R), BF),
     gate=((H, NIB, J, D, 128), F32), gated=((NIB, J, H, D, 128), BF), const=((192, 256), BF), fill_rows=((64, R), BF), weights=((5 * C, C), BF),
-    bias_kt=((2 * R, 128), BF), logits=((2, 2 * R, 256), F32))
+    bias_kt=((2 * R, 128), BF), logits=((2, 2 * R, 256), F32), best=((2, 1, 256), F32))
 
 
 def solution(mesh):
     def body(pair_tile, res_mask, ln_gamma, ln_beta, w_q, w_k, w_v, w_b, w_g, w_o):
         pair_t = jnp.transpose(pair_tile, (1, 2, 0))
         scratch = [pltpu.VMEM(shape, dtype) for shape, dtype in SCRATCH.values()]
-        sems = [pltpu.SemaphoreType.DMA((n,)) for n in (H * 36, H * 36, 2, 1, 2 * H, 2 * H)]
+        sems = [pltpu.SemaphoreType.DMA((n,)) for n in (H * 36, H * 36, 4, 2, 2 * H, 2 * H)]
         out_t = pl.pallas_call(
             kernel,
             out_shape=jax.ShapeDtypeStruct((J, C, R), BF),

time: 83.1 us -> 69.9 us (0.84)
  Pallas kernels: 80.6 us -> 67.4 us
    pallas_call x1, Pallas kernels: 80.6 us -> 67.4 us  [body(): pl.pallas_call(kernel, out_shape=jax.ShapeDtypeStruct((J, C, R), BF), in_...]
where the time goes in v3:
time: 69.9 us; the launch traced here: 69.7 us
  Pallas kernels  67.4 us (96%)
  local copies, waits for them, and re-layouts  2.29 us (3%)
    pallas_call x1, Pallas kernels, body(): pl.pallas_call(kernel, out_shape=jax.ShapeDtypeStruct((J, C, R), BF), in_...  67.4 us
    unnamed x1, local copies, waits for them, and re-layouts  2.29 us

profile of v3, /device:TPU:1, one launch (start us, length us, event | category | flops | bytes accessed | tf_op | source)
XLA Modules:
  0.0 69.7 jit_solution(1274711005888723784)
XLA Ops:
  0.0 67.4 %shard_map.100 = bf16[16,64,512]{2,1,0:T(8,128)(2,1)} custom-call(bf16[16,64,512]{2,1,0:T(8,128)(2,1)} %bitcast.7, s32[8,128]{1,0:T(8,128)} %bitcast.8, f32[1,64]{1,0:T(1,128)} %bitcast.10, f32[1,64]{1,0:T(1,128)} %bitcast.11, bf16[64,64]{1,0:T(8,128)(2,1)} %wq_ref.1, bf16[64,64]{1,0:T(8,128)(2,1)} %wk_ref.1, bf16[64,64]{1,0:T(8,128)(2,1)} %wv_ref.1, ...), custom_call_target="tpu_custom_call" | custom-call | tf_op jit(solution)/shard_map/pallas_call | solution.py:360
  67.4 2.3 %copy.12 = bf16[512,16,64]{0,2,1:T(8,128)(2,1)} copy(bf16[512,16,64]{0,2,1:T(8,128)(2,1)} %bitcast.6) | data formatting | bytes 2097152

commit v4 on v3

--- a/solution.py
+++ b/solution.py
@@ -19,11 +19,13 @@
 
 
 class Gather:
-    def __init__(self, bias_all, send_sem, recv_sem):
-        self.bufs, self.send_sem, self.recv_sem = bias_all, send_sem, recv_sem
+    def __init__(self, bias_own, bias_all, spare, send_sem, recv_sem, plane_send, plane_recv, own_send):
+        self.own, self.bufs, self.spare, self.send_sem, self.recv_sem = bias_own, bias_all, spare, send_sem, recv_sem
+        self.plane_sem, self.plane_recv, self.own_sem = plane_send, plane_recv, own_send
         self.col, self.row = lax.axis_index("col"), lax.axis_index("row")
         self.z, self.y, self.x = self.col // 16, (self.col // 4) % 4, self.col % 4
         self.turn = (self.z - 2 * self.row + 4) % 4
+        self.owner = self.z // 2
         self.source = self.turn < 2
 
     def neighbour(self, dim, step):
@@ -39,48 +41,64 @@
     def here(self, dim):
         return {"z": self.z % 2, "y": self.y, "x": self.x}[dim]
 
-    def copy(self, head, part, phase, slot, value, half, step):
+    def pieces(self, head, act):
+        for r, own in enumerate((((0, 0, 0, 3), (3, 1, 0, 1)), ((0, 1, 1, 2), (2, 2, 0, 2)))):
+            for tiles, part, lo, size in own:
+                order, sem = ORDERS[part], head * 3 + part
+                src = self.own.at[head, pl.ds(tiles, size)]
+                dst = self.bufs[part].at[(head, *(self.here(dim) for dim in reversed(order)), pl.ds(lo, size))]
+
+                def away(device, src=src, dst=dst, sem=sem, send=self.plane_sem):
+                    return pltpu.make_async_remote_copy(src_ref=src, dst_ref=dst, send_sem=send.at[sem], recv_sem=self.plane_recv.at[sem], device_id=device, device_id_type=MESH)
+
+                def start():
+                    @pl.loop(1, 16)
+                    def _(n):
+                        at = {"z": self.z, "y": self.y, "x": self.x}
+                        for dim, step in zip(order[:2], (n % 4, n // 4)):
+                            at[dim] = (at[dim] + step) % 4
+                        away({"col": (at["z"] * 4 + at["y"]) * 4 + at["x"], "row": self.owner}).start()
+
+                def wait():
+                    ref = self.spare.at[pl.ds(0, 15 * size)]
+                    away({"row": 1 - self.row}, ref, ref).wait_send()
+
+                def stay():
+                    pltpu.make_async_copy(src, dst, self.plane_recv.at[sem]).start()
+
+                def cross():
+                    copy = away({"row": 1 - self.row}, send=self.own_sem)
+                    copy.start() if act == "start" else copy.wait_send()
+
+                pl.when(self.row == r)(start if act == "start" else wait)
+                pl.when((self.row == r) & (self.owner != r))(cross)
+                if act == "start":
+                    pl.when((self.row == r) & (self.owner == r))(stay)
+
+    def arrived(self, head):
+        for part in range(3):
+            ref = self.bufs[part].at[head, self.here(ORDERS[part][2])]
+            wait = pltpu.make_async_remote_copy(src_ref=ref, dst_ref=ref, send_sem=self.own_sem.at[0], recv_sem=self.plane_recv.at[head * 3 + part], device_id={"row": 1 - self.row}, device_id_type=MESH).wait_recv
+            pl.when(self.source)(wait) if part == 0 else wait()
+
+    def copy(self, head, part, slot, value, half, step):
         order = ORDERS[part]
-        pos = {}
-        for n, dim in enumerate(order):
-            pos[dim] = slice(None) if n < phase else value if n == phase else self.here(dim)
+        middle = slice(None)
         if half is not None:
             size = 1 if order[1] == "z" else 2
-            pos[order[1]] = pl.ds(half * size, size)
-        ref = self.bufs[part].at[(head, pos[order[2]], pos[order[1]], pos[order[0]])]
-        sem = ((head * 3 + part) * 3 + phase) * 4 + slot
-        return pltpu.make_async_remote_copy(src_ref=ref, dst_ref=ref, send_sem=self.send_sem.at[sem], recv_sem=self.recv_sem.at[sem], device_id=self.neighbour(order[phase], step), device_id_type=MESH)
-
-    def among(self, part, phase, go):
-        pl.when(self.source)(go) if "z" in ORDERS[part][phase:] else go()
-
-    def first(self, head, phase, act="start"):
+            middle = pl.ds(half * size, size)
+        ref = self.bufs[part].at[head, value, middle]
+        sem = (head * 3 + part) * 4 + slot
+        return pltpu.make_async_remote_copy(src_ref=ref, dst_ref=ref, send_sem=self.send_sem.at[sem], recv_sem=self.recv_sem.at[sem], device_id=self.neighbour(order[2], step), device_id_type=MESH)
+
+    def first(self, head, act="start"):
         for part in range(3):
 
             def go():
-                for slot, step in ((0, 1), (1, -1), (2, 2))[: 2 if phase == 2 else 3]:
-                    getattr(self.copy(head, part, phase, slot, self.here(ORDERS[part][phase]), None, step), act)()
-
-            self.among(part, phase, go)
-
-    def arrived(self, head, phase):
-        for part in range(3):
-            dim = ORDERS[part][phase]
-            if dim == "z":
-                for turn, waits in enumerate((((1, 1),), ((0, 0),), ((0, 1), (2, 0)), ((1, 0), (2, 1)))):
-
-                    @pl.when(self.turn == turn)
-                    def _():
-                        for slot, value in waits:
-                            self.copy(head, part, phase, slot, value, None, 1).wait_recv()
-
-                continue
-
-            def go():
-                for slot, back in ((0, 3), (1, 1), (2, 2)):
-                    self.copy(head, part, phase, slot, (self.here(dim) + back) % 4, None, 1).wait_recv()
-
-            self.among(part, phase, go)
+                for slot, step in ((0, 1), (1, -1)):
+                    getattr(self.copy(head, part, slot, self.here(ORDERS[part][2]), None, step), act)()
+
+            pl.when(self.source)(go) if part == 0 else go()
 
     def relay(self, head, act="start"):
         for part in range(3):
@@ -92,15 +110,15 @@
                     @pl.when(self.turn == turn)
                     def _():
                         if act == "start":
-                            self.copy(head, part, 2, slot, value, None, 1).wait_recv()
-                        getattr(self.copy(head, part, 2, out, value, half, step), act)()
+                            self.copy(head, part, slot, value, None, 1).wait_recv()
+                        getattr(self.copy(head, part, out, value, half, step), act)()
 
                 continue
             for slot, back, half, step in ((0, 3, 0, 1), (1, 1, 1, -1)):
                 value = (self.here(dim) + back) % 4
                 if act == "start":
-                    self.copy(head, part, 2, slot, value, None, 1).wait_recv()
-                getattr(self.copy(head, part, 2, slot + 2, value, half, step), act)()
+                    self.copy(head, part, slot, value, None, 1).wait_recv()
+                getattr(self.copy(head, part, slot + 2, value, half, step), act)()
 
     def finish(self, head):
         for part in range(3):
@@ -111,34 +129,37 @@
                     @pl.when(self.turn == turn)
                     def _():
                         for slot, half in slots:
-                            self.copy(head, part, 2, slot, value, half, 1).wait_recv()
+                            self.copy(head, part, slot, value, half, 1).wait_recv()
 
                 continue
             for slot, half in ((2, 0), (3, 1)):
-                self.copy(head, part, 2, slot, (self.here(dim) + 2) % 4, half, 1).wait_recv()
-
-    def step1(self, head):
-        self.arrived(head, 0)
-        self.first(head, 1)
-
-    def step2(self, head):
-        self.arrived(head, 1)
-        self.first(head, 2)
+                self.copy(head, part, slot, (self.here(dim) + 2) % 4, half, 1).wait_recv()
+
+    def forward(self, head):
+        self.arrived(head)
+        self.first(head)
 
 
 def kernel(pair_ref, mask_ref, gamma_ref, beta_ref, wq_ref, wk_ref, wv_ref, wg_ref, wbt_ref, wo_ref, out_ref,
-           normed, bias_f32, bias_own, bias_a, bias_b, bias_c, query, keys_t, keys, values, gate, gated, const, fill_rows, weights, bias_kt, logits, best,
-           send_sem, recv_sem, own_send, own_recv, kv_send, kv_recv):
+           normed, bias_f32, bias_own, spare, bias_a, bias_b, bias_c, query, keys_t, keys, values, gate, gated, const, fill_rows, weights, bias_kt, logits, best,
+           send_sem, recv_sem, plane_send, plane_recv, own_send, kv_send, kv_recv):
     row = lax.axis_index("row")
     bias_all = (bias_a, bias_b, bias_c)
-    gather = Gather(bias_all, send_sem, recv_sem)
-    owner = gather.z // 2
+    gather = Gather(bias_own, bias_all, spare, send_sem, recv_sem, plane_send, plane_recv, own_send)
     partner = {"row": 1 - row}
 
     barrier = pltpu.get_barrier_semaphore()
-    peers = [partner] + [gather.neighbour(dim, step) for dim in "xyz" for step in (1, -1, 2)]
-    for peer in peers:
-        pl.semaphore_signal(barrier, inc=1, device_id=peer, device_id_type=MESH)
+    pl.semaphore_signal(barrier, inc=1, device_id=partner, device_id_type=MESH)
+
+    @pl.loop(1, 64)
+    def _(n):
+        dz, dy, dx = n // 16, n // 4 % 4, n % 4
+
+        @pl.when((dz == 0) | (dy == 0) | (dx == 0))
+        def _():
+            col = ((gather.z + dz) % 4 * 4 + (gather.y + dy) % 4) * 4 + (gather.x + dx) % 4
+            for r in range(2):
+                pl.semaphore_signal(barrier, inc=1, device_id={"col": col, "row": r}, device_id_type=MESH)
 
     diag = lax.broadcasted_iota(jnp.int32, (C, C), 0) == lax.broadcasted_iota(jnp.int32, (C, C), 1)
     gamma = jnp.sum(jnp.where(diag, gamma_ref[...], 0.0), axis=1, keepdims=True)
@@ -158,36 +179,10 @@
         for t in range(4):
             bias_own[h, t] = bias_f32[h, :, t * 128:(t + 1) * 128].astype(BF)
 
-    pl.semaphore_wait(barrier, len(peers))
-
-    def own_copies(r):
-        for tiles, part, lo, size in (((0, 0, 0, 3), (3, 1, 0, 1)), ((0, 1, 1, 2), (2, 2, 0, 2)))[r]:
-            place = tuple(gather.here(dim) for dim in reversed(ORDERS[part]))
-            yield bias_own.at[:, pl.ds(tiles, size)], bias_all[part].at[(slice(None), *place, pl.ds(lo, size))]
-
-    def own_away(r):
-        for n, (src, dst) in enumerate(own_copies(r)):
-            yield pltpu.make_async_remote_copy(src_ref=src, dst_ref=dst, send_sem=own_send.at[n], recv_sem=own_recv.at[n], device_id=partner, device_id_type=MESH)
-
-    for r in range(2):
-
-        @pl.when((row == r) & (owner != r))
-        def _():
-            for copy in own_away(r):
-                copy.start()
-
-        @pl.when((row == r) & (owner == r))
-        def _():
-            stays = [pltpu.make_async_copy(src, dst, own_send.at[2 + n]) for n, (src, dst) in enumerate(own_copies(r))]
-            for copy in stays:
-                copy.start()
-            for copy in stays:
-                copy.wait()
-            for copy in own_away(1 - r):
-                copy.wait_recv()
-
-    for h in range(H):
-        gather.first(h, 0)
+    pl.semaphore_wait(barrier, 73)
+
+    gather.pieces(0, "start")
+    gather.pieces(1, "start")
 
     rows_i = lax.broadcasted_iota(jnp.int32, (64, 256), 0)
     const[0:64, :] = jnp.where(rows_i < 3, 1.0, 0.0).astype(BF)
@@ -228,17 +223,16 @@
         for n, ref in enumerate((keys.at[r, pl.ds(h * 4, 4)], values.at[r, h])):
             yield pltpu.make_async_remote_copy(src_ref=ref, dst_ref=ref, send_sem=kv_send.at[h * 2 + n], recv_sem=kv_recv.at[h * 2 + n], device_id=partner, device_id_type=MESH)
 
-    lax.fori_loop(0, 8, project, 0)
-    gather.step1(0)
-    lax.fori_loop(8, 16, project, 0)
-    gather.step2(0)
-    gather.step1(1)
+    lax.fori_loop(0, 16, project, 0)
+    gather.forward(0)
     lax.fori_loop(0, 16, turn_keys, 0)
     for h in range(H):
         for copy in kv_copies(h, row):
             copy.start()
     gather.relay(0)
-    gather.step2(1)
+    gather.forward(1)
+    gather.pieces(2, "start")
+    schedule = ((1, gather.relay, 1), (2, gather.forward, 2), (3, lambda h: gather.pieces(h, "start"), 3), (5, gather.relay, 2), (7, gather.forward, 3), (10, gather.relay, 3))
 
     logits[1] = jnp.zeros((2 * R, 256), F32)
     best[1] = jnp.zeros((1, 256), F32)
@@ -253,17 +247,8 @@
                 copy.wait_recv()
             gather.finish(h)
 
-        @pl.when((ib == 0) & (h < H - 2))
-        def _():
-            gather.step1(h + 2)
-
-        @pl.when((ib == 1) & (h < H - 1))
-        def _():
-            gather.relay(h + 1)
-
-        @pl.when((ib == 2) & (h < H - 2))
-        def _():
-            gather.step2(h + 2)
+        for unit, step, head in schedule:
+            pl.when(n == unit)(functools.partial(step, head))
 
         last = jnp.maximum(n - 1, 0)
         attend(h, ib, (last // NIB, last % NIB), bias_all, query, keys, values, gate, gated, const, bias_kt, logits, best)
@@ -273,18 +258,11 @@
 
     @pl.loop(0, H)
     def _(h):
-        for phase in range(3):
-            gather.first(h, phase, "wait_send")
+        gather.pieces(h, "wait")
+        gather.first(h, "wait_send")
         gather.relay(h, "wait_send")
         for copy in kv_copies(h, row):
             copy.wait_send()
-
-    for r in range(2):
-
-        @pl.when((row == r) & (owner != r))
-        def _():
-            for copy in own_away(r):
-                copy.wait_send()
 
 
 def mix(p, h, ib, values, gate, gated, logits, best):
@@ -346,7 +324,7 @@
 
 
 SCRATCH = dict(
-    normed=((J, C, R), BF), bias_f32=((H, J, R), F32), bias_own=((H, 4, J, 128), BF), bias_a=((H, 2, 4, 4, 3, J, 128), BF), bias_b=((H, 4, 2, 4, 3, J, 128), BF), bias_c=((H, 4, 4, 2, 2, J, 128), BF),
+    normed=((J, C, R), BF), bias_f32=((H, J, R), F32), bias_own=((H, 4, J, 128), BF), spare=((45, J, 128), BF), bias_a=((H, 2, 4, 4, 3, J, 128), BF), bias_b=((H, 4, 2, 4, 3, J, 128), BF), bias_c=((H, 4, 4, 2, 2, J, 128), BF),
     query=((H, NIB, J, D, 128), BF), keys_t=((H, J, D, R), BF), keys=((2, 16, R, 128), BF), values=((2, H, J, D, R), BF),
     gate=((H, NIB, J, D, 128), F32), gated=((NIB, J, H, D, 128), BF), const=((192, 256), BF), fill_rows=((64, R), BF), weights=((5 * C, C), BF),
     bias_kt=((2 * R, 128), BF), logits=((2, 2 * R, 256), F32), best=((2, 1, 256), F32))
@@ -356,7 +334,7 @@
     def body(pair_tile, res_mask, ln_gamma, ln_beta, w_q, w_k, w_v, w_b, w_g, w_o):
         pair_t = jnp.transpose(pair_tile, (1, 2, 0))
         scratch = [pltpu.VMEM(shape, dtype) for shape, dtype in SCRATCH.values()]
-        sems = [pltpu.SemaphoreType.DMA((n,)) for n in (H * 36, H * 36, 4, 2, 2 * H, 2 * H)]
+        sems = [pltpu.SemaphoreType.DMA((n,)) for n in (H * 12, H * 12, H * 3, H * 3, H * 3, 2 * H, 2 * H)]
         out_t = pl.pallas_call(
             kernel,
             out_shape=jax.ShapeDtypeStruct((J, C, R), BF),

time: 69.9 us -> 69.5 us (level)
  no operation moved by 1% of the time
where the time goes in v4:
time: 69.5 us; the launch traced here: 69.4 us
  Pallas kernels  67.1 us (97%)
  local copies, waits for them, and re-layouts  2.29 us (3%)
    pallas_call x1, Pallas kernels, body(): pl.pallas_call(kernel, out_shape=jax.ShapeDtypeStruct((J, C, R), BF), in_...  67.1 us
    unnamed x1, local copies, waits for them, and re-layouts  2.29 us

profile of v4, /device:TPU:1, one launch (start us, length us, event | category | flops | bytes accessed | tf_op | source)
XLA Modules:
  0.0 69.4 jit_solution(18427426924667255653)
XLA Ops:
  0.0 67.1 %shard_map.100 = bf16[16,64,512]{2,1,0:T(8,128)(2,1)} custom-call(bf16[16,64,512]{2,1,0:T(8,128)(2,1)} %bitcast.7, s32[8,128]{1,0:T(8,128)} %bitcast.8, f32[1,64]{1,0:T(1,128)} %bitcast.10, f32[1,64]{1,0:T(1,128)} %bitcast.11, bf16[64,64]{1,0:T(8,128)(2,1)} %wq_ref.1, bf16[64,64]{1,0:T(8,128)(2,1)} %wk_ref.1, bf16[64,64]{1,0:T(8,128)(2,1)} %wv_ref.1, ...), custom_call_target="tpu_custom_call" | custom-call | tf_op jit(solution)/shard_map/pallas_call | solution.py:338
  67.1 2.3 %copy.12 = bf16[512,16,64]{0,2,1:T(8,128)(2,1)} copy(bf16[512,16,64]{0,2,1:T(8,128)(2,1)} %bitcast.6) | data formatting | bytes 2097152

commit v5 on v4

--- a/solution.py
+++ b/solution.py
@@ -182,7 +182,6 @@
     pl.semaphore_wait(barrier, 73)
 
     gather.pieces(0, "start")
-    gather.pieces(1, "start")
 
     rows_i = lax.broadcasted_iota(jnp.int32, (64, 256), 0)
     const[0:64, :] = jnp.where(rows_i < 3, 1.0, 0.0).astype(BF)
@@ -224,15 +223,23 @@
             yield pltpu.make_async_remote_copy(src_ref=ref, dst_ref=ref, send_sem=kv_send.at[h * 2 + n], recv_sem=kv_recv.at[h * 2 + n], device_id=partner, device_id_type=MESH)
 
     lax.fori_loop(0, 16, project, 0)
-    gather.forward(0)
-    lax.fori_loop(0, 16, turn_keys, 0)
-    for h in range(H):
+    def kv_start(h):
         for copy in kv_copies(h, row):
             copy.start()
+
+    def scatter(h):
+        gather.pieces(h, "start")
+
+    gather.forward(0)
+    scatter(1)
+    lax.fori_loop(0, 16, turn_keys, 0)
+    kv_start(0)
     gather.relay(0)
     gather.forward(1)
-    gather.pieces(2, "start")
-    schedule = ((1, gather.relay, 1), (2, gather.forward, 2), (3, lambda h: gather.pieces(h, "start"), 3), (5, gather.relay, 2), (7, gather.forward, 3), (10, gather.relay, 3))
+    scatter(2)
+    schedule = (
+        (0, kv_start, 1), (1, gather.relay, 1), (1, scatter, 3), (1, kv_start, 2), (2, gather.forward, 2), (2, kv_start, 3),
+        (5, gather.relay, 2), (5, gather.forward, 3), (8, gather.relay, 3))
 
     logits[1] = jnp.zeros((2 * R, 256), F32)
     best[1] = jnp.zeros((1, 256), F32)
@@ -268,10 +275,11 @@
 def mix(p, h, ib, values, gate, gated, logits, best):
     total = jnp.zeros((1, 256), F32)
     acc = None
-    for kh in range(2):
-        e = jnp.exp2((logits[p % 2, kh * R:(kh + 1) * R, :] - best[p % 2]) * LOG2E)
+    for q in range(4):
+        e = jnp.exp2((logits[p % 2, q * 256:q * 256 + 256, :] - best[p % 2]) * LOG2E)
         total = total + jnp.sum(e, axis=0, keepdims=True)
-        v = jnp.concatenate([values[kh, h, 2 * p], values[kh, h, 2 * p + 1]], axis=0)
+        vs = slice((q % 2) * 256, (q % 2) * 256 + 256)
+        v = jnp.concatenate([values[q // 2, h, 2 * p, :, vs], values[q // 2, h, 2 * p + 1, :, vs]], axis=0)
         o = jnp.dot(v, e.astype(BF), preferred_element_type=F32)
         acc = o if acc is None else acc + o
     scale = 1.0 / total
@@ -298,10 +306,11 @@
         top = [gap, gap, left, right] if odd else [left, right, gap, gap]
         rhs = jnp.concatenate(top + [const[...]], axis=0)
         high = None
-        for kh in range(2):
-            lhs = jnp.concatenate([keys[kh, h * 4 + group], bias_kt[kh * R:(kh + 1) * R, :]], axis=1)
+        for q in range(4):
+            rs = slice(q * 256, q * 256 + 256)
+            lhs = jnp.concatenate([keys[q // 2, h * 4 + group, (q % 2) * 256:(q % 2) * 256 + 256, :], bias_kt[rs, :]], axis=1)
             s = jnp.dot(lhs, rhs, preferred_element_type=F32)
-            logits[p % 2, kh * R:(kh + 1) * R, :] = s
+            logits[p % 2, rs, :] = s
             m = jnp.max(s, axis=0, keepdims=True)
             high = m if high is None else jnp.maximum(high, m)
         best[p % 2] = high

time: 69.5 us -> 69.5 us (level)
  no operation moved by 1% of the time
where the time goes in v5:
time: 69.5 us; the launch traced here: 69.1 us
  Pallas kernels  66.8 us (96%)
  local copies, waits for them, and re-layouts  2.29 us (3%)
    pallas_call x1, Pallas kernels, body(): pl.pallas_call(kernel, out_shape=jax.ShapeDtypeStruct((J, C, R), BF), in_...  66.8 us
    unnamed x1, local copies, waits for them, and re-layouts  2.29 us

profile of v5, /device:TPU:1, one launch (start us, length us, event | category | flops | bytes accessed | tf_op | source)
XLA Modules:
  0.0 69.1 jit_solution(8849885502646395560)
XLA Ops:
  0.0 66.8 %shard_map.100 = bf16[16,64,512]{2,1,0:T(8,128)(2,1)} custom-call(bf16[16,64,512]{2,1,0:T(8,128)(2,1)} %bitcast.7, s32[8,128]{1,0:T(8,128)} %bitcast.8, f32[1,64]{1,0:T(1,128)} %bitcast.10, f32[1,64]{1,0:T(1,128)} %bitcast.11, bf16[64,64]{1,0:T(8,128)(2,1)} %wq_ref.1, bf16[64,64]{1,0:T(8,128)(2,1)} %wk_ref.1, bf16[64,64]{1,0:T(8,128)(2,1)} %wv_ref.1, ...), custom_call_target="tpu_custom_call" | custom-call | tf_op jit(solution)/shard_map/pallas_call | solution.py:347
  66.8 2.3 %copy.12 = bf16[512,16,64]{0,2,1:T(8,128)(2,1)} copy(bf16[512,16,64]{0,2,1:T(8,128)(2,1)} %bitcast.6) | data formatting | bytes 2097152
